TPU v7x, 512 devices: a 4x2x32 block of a 4x8x32 slice. The times are simulated.
512 devices in a mesh: members: 2 (over y), patch: 64 (over z, core), feat: 4 (over x).
Axes of the slice: x: 4, y: 2, z: 32, core: 2. Of those that a mesh axis runs over, the one named last changes fastest.
The devices are a block of a 4x8x32 slice.
Arguments:
- latents: bfloat16 [393216, 512], P(('members', 'patch', 'feat')), parts along dimension 0, may hold values from -6 to 6
- neighbours: int32 [196608, 8], P(('patch', 'feat')), may hold values from 0 to 1279
- degree: int32 [196608], P(('patch', 'feat')), may hold values from 4 to 8
- send_rows: int32 [16384, 8], P(('patch', 'feat')), may hold values from 0 to 767
- area: float32 [196608], P(('patch', 'feat')), may hold values from 0.3 to 10
- scenario: int32 [6], P('members'), parts along dimension 0, may hold values from 0 to 15
- totals: float32 [16, 3], replicated, may hold values from 0.3 to 1.5
- w_send: bfloat16 [1, 512, 512], P(None, None, 'feat'), may hold values from -0.25 to 0.25
- w_recv: bfloat16 [1, 512, 512], P(None, None, 'feat'), may hold values from -0.25 to 0.25
- b_edge: float32 [1, 512], replicated, may hold values from -3 to 3
- w_msg: bfloat16 [1, 512, 512], P(None, None, 'feat'), may hold values from -0.25 to 0.25
- w_node: bfloat16 [1, 1024, 512], P(None, None, 'feat'), may hold values from -0.1875 to 0.1875
- w_out: bfloat16 [1, 512, 512], P(None, None, 'feat'), may hold values from -0.25 to 0.25
- gain: float32 [1, 512], replicated, may hold values from 0.5 to 1.5
- w_dec: bfloat16 [3, 512], replicated, may hold values from -0.25 to 0.25
- w_enc: float32 [3, 512], replicated, may hold values from -3 to 3
Outputs:
- final_latents: bfloat16 [393216, 512], P(('members', 'patch', 'feat')), parts along dimension 0
- conserved: float32 [4, 3, 196608], P('members', None, ('patch', 'feat')), parts along dimension 0
There are 2 independent parts, one for each index of `members`. A program takes and returns all parts, laid end to end along the dimension named above; an argument that names none is the same for every part. Nothing has to cross between parts.
Inputs may be any that keep to these rules, and one draw needn't show every extreme that they name: `neighbours`: an entry below 768 is a row of the node's own device; entry 768 + j * 8 + t names the t-th row that the device of patch j with the same feat index sends to the node's patch. A node's live slots are its first degree[n] slots. `send_rows`: row q * 64 + i lists rows of device q, in its own numbering, that patch i receives.
All inputs are finite; a program needn't handle non-finite values.
Results may differ from a plain program's by a relative error of at most 0.012.
Values may be sent and summed in bfloat16 or wider, within the bound.
A program may use at most 64 MiB of HBM per device.

v0:
```python
import jax
import jax.numpy as jnp
from jax import lax
from jax.sharding import Mesh
from jax.sharding import PartitionSpec as P

STEPS = 2
PATCH = ("patch_0", "patch_1")
PATCH_FEAT = ("patch_0", "patch_1", "feat")
MEMBERS_PATCH_FEAT = ("members", "patch_0", "patch_1", "feat")


EPSILON = 1e-05


def over_axes(x, axes):
    for axis in axes:
        x = lax.psum(x, axis)
    return x


def node_terms(rows, message, width, piece):
    return jnp.dot(rows, piece[:width], preferred_element_type=jnp.float32) + jnp.dot(
        message, piece[width:], preferred_element_type=jnp.float32
    )


def shards(
    latents,
    neighbours,
    degree,
    send_rows,
    area,
    scenario,
    totals,
    w_send,
    w_recv,
    b_edge,
    w_msg,
    w_node,
    w_out,
    gain,
    w_dec,
    w_enc,
):
    width = latents.shape[1]
    node_count = float(area.shape[0] * lax.axis_size(PATCH) * lax.axis_size("feat"))
    live_slots = jnp.arange(neighbours.shape[1], dtype=jnp.int32)[None, :] < degree[:, None]
    chosen = (jnp.arange(totals.shape[0], dtype=jnp.int32)[:, None] == scenario[None, :]).astype(
        jnp.float32
    )
    target = jnp.sum(chosen * totals, axis=0)
    kept = (
        lax.all_gather(w_send, "feat", axis=2, tiled=True),
        lax.all_gather(w_recv, "feat", axis=2, tiled=True),
        lax.all_gather(w_msg, "feat", axis=2, tiled=True),
        lax.all_gather(w_node, "feat", axis=2, tiled=True),
        lax.all_gather(w_out, "feat", axis=2, tiled=True),
    )
    latent_state = latents
    history = []
    for step_index in range(STEPS):
        sender = jnp.dot(latent_state, kept[0][0], preferred_element_type=jnp.float32).astype(
            jnp.bfloat16
        )
        receiver = jnp.dot(latent_state, kept[1][0], preferred_element_type=jnp.float32)
        receiver = receiver + b_edge[0][None, :]
        outgoing = sender[send_rows]
        incoming = lax.all_to_all(outgoing, PATCH, split_axis=0, concat_axis=0, tiled=True)
        table = jnp.concatenate([sender, incoming.reshape(-1, width)], axis=0)
        summed = jnp.zeros(receiver.shape, jnp.float32)
        for position in range(neighbours.shape[1]):
            edge_value = table[neighbours[:, position]].astype(jnp.float32) + receiver
            summed = summed + jnp.where(
                live_slots[:, position : position + 1], jax.nn.silu(edge_value), 0.0
            )
        summed = summed.astype(jnp.bfloat16)
        message = jnp.dot(summed, kept[2][0], preferred_element_type=jnp.float32).astype(
            jnp.bfloat16
        )
        pre_hidden = node_terms(latent_state, message, width, kept[3][0])
        hidden = jax.nn.silu(pre_hidden).astype(jnp.bfloat16)
        output = jnp.dot(hidden, kept[4][0], preferred_element_type=jnp.float32)
        average = jnp.mean(output, axis=1, keepdims=True)
        variance = jnp.mean(jnp.square(output - average), axis=1, keepdims=True)
        normed = (output - average) * lax.rsqrt(variance + EPSILON) * gain[0][None, :]
        latent_state = (latent_state.astype(jnp.float32) + normed).astype(jnp.bfloat16)
        decoded = lax.dot_general(
            w_dec, latent_state, (((1,), (1,)), ((), ())), preferred_element_type=jnp.float32
        )
        fields = jax.nn.softplus(decoded)
        integral = over_axes(jnp.sum(area[None, :] * fields, axis=1), PATCH_FEAT)
        scale = target * node_count / integral
        history.append(scale[:, None] * fields)
        change = (scale - 1.0)[:, None] * fields
        update = lax.dot_general(
            change, w_enc, (((0,), (0,)), ((), ())), preferred_element_type=jnp.float32
        )
        latent_state = (latent_state.astype(jnp.float32) + update).astype(jnp.bfloat16)
    return (latent_state, jnp.stack(history))


def solution(mesh):
    split = Mesh(
        mesh.devices.reshape(mesh.shape["members"], 32, 2, mesh.shape["feat"]),
        ("members", "patch_0", "patch_1", "feat"),
    )
    placed = (
        P(MEMBERS_PATCH_FEAT, None),
        P(PATCH_FEAT, None),
        P(PATCH_FEAT),
        P(PATCH_FEAT, None),
        P(PATCH_FEAT),
        P("members"),
        P(),
        P(None, None, "feat"),
        P(None, None, "feat"),
        P(),
        P(None, None, "feat"),
        P(None, None, "feat"),
        P(None, None, "feat"),
        P(),
        P(),
        P(),
    )
    return jax.shard_map(
        shards,
        mesh=split,
        in_specs=placed,
        out_specs=(P(MEMBERS_PATCH_FEAT, None), P("members", None, PATCH_FEAT)),
        check_vma=False,
    )
```

profile of v0, /device:TPU:33, one launch (start us, length us, event | category | flops | bytes accessed | tf_op | source)
XLA Modules:
  0.0 436.3 jit_solution(16447219351764696672)
XLA Ops:
  8.1 12.8 %all_gather.16 = bf16[1,512,512]{2,1,0:T(8,128)(2,1)S(1)} all-gather(bf16[1,512,128]{2,1,0:T(8,128)(2,1)} %param.23), channel_id=1, replica_groups=mesh['members'=2,'patch_0'=32,'patch_1'=2,'feat'=4] {'feat'}, dimensions={2}, use_global_device_ids=true | all-gather | bytes 655360 | tf_op jit(solution)/shard_map/all_gather | solution.py:54
  26.1 49.8 %all-to-all-start = ((bf16[64,8,512]{2,1,0:T(8,128)(2,1)}), bf16[64,8,512]{2,1,0:T(8,128)(2,1)S(1)}, u32[]{:S(2)}, u32[]{:S(2)}) async-start(bf16[64,8,512]{2,1,0:T(8,128)(2,1)} %bitcast.2), calls=%async_computation | async-start | bytes 1048576 | tf_op jit(solution)/shard_map/all_to_all | solution.py:69
  78.1 12.3 %all_gather.17 = bf16[1,512,512]{2,1,0:T(8,128)(2,1)} all-gather(bf16[1,512,128]{2,1,0:T(8,128)(2,1)S(1)} %copy-done.8), channel_id=1, replica_groups=mesh['members'=2,'patch_0'=32,'patch_1'=2,'feat'=4] {'feat'}, dimensions={2}, use_global_device_ids=true | all-gather | bytes 655360 | tf_op jit(solution)/shard_map/all_gather | solution.py:55
  90.5 10.9 %all_gather.18 = bf16[1,512,512]{2,1,0:T(8,128)(2,1)} all-gather(bf16[1,512,128]{2,1,0:T(8,128)(2,1)S(1)} %copy-done.9), channel_id=1, replica_groups=mesh['members'=2,'patch_0'=32,'patch_1'=2,'feat'=4] {'feat'}, dimensions={2}, use_global_device_ids=true | all-gather | bytes 655360 | tf_op jit(solution)/shard_map/all_gather | solution.py:56
  101.4 16.3 %all_gather.19 = bf16[1,512,512]{2,1,0:T(8,128)(2,1)} all-gather(bf16[1,512,128]{2,1,0:T(8,128)(2,1)S(1)} %copy-done.10), channel_id=1, replica_groups=mesh['members'=2,'patch_0'=32,'patch_1'=2,'feat'=4] {'feat'}, dimensions={2}, use_global_device_ids=true | all-gather | bytes 655360 | tf_op jit(solution)/shard_map/all_gather | solution.py:58
  117.7 5.8 %all-gather.2.cloned.1.call-done = bf16[1,1024,512]{2,1,0:T(8,128)(2,1)} async-done(((bf16[1,1024,128]{2,1,0:T(8,128)(2,1)}), bf16[1,1024,512]{2,1,0:T(8,128)(2,1)}) %all-gather.2.cloned.1.call-update) | async-done | bytes 1048592 | tf_op jit(solution)/shard_map/all_gather | solution.py:57
  126.2 13.6 %all-to-all-done = bf16[64,8,512]{2,1,0:T(8,128)(2,1)S(1)} async-done(((bf16[64,8,512]{2,1,0:T(8,128)(2,1)}), bf16[64,8,512]{2,1,0:T(8,128)(2,1)S(1)}, u32[]{:S(2)}, u32[]{:S(2)}) %all-to-all-start) | async-done | bytes 524320 | tf_op jit(solution)/shard_map/all_to_all | solution.py:69
  142.6 3.3 gather_fusion.7
  146.0 3.3 gather_fusion.6
  149.3 3.3 gather_fusion.5
  152.6 3.3 gather_fusion.4
  155.9 3.3 gather_fusion.3
  159.3 3.3 gather_fusion.2
  162.6 3.5 gather_fusion.1
  166.1 8.3 %convolution_convert_fusion.2 = bf16[768,512]{1,0:T(8,128)(2,1)} fusion(bf16[768,512]{1,0:T(8,128)(2,1)S(1)} %gather_fusion.8, bf16[768,512]{1,0:T(8,128)(2,1)} %gather_fusion.7, bf16[768,512]{1,0:T(8,128)(2,1)} %gather_fusion.6, bf16[768,512]{1,0:T(8,128)(2,1)} %gather_fusion.5, bf16[768,512]{1,0:T(8,128)(2,1)} %gather_fusion.4, ...), kind=kOutput, calls=%fused_computation.30 | convolution fusion | flops 831258624 | bytes 8921088 | tf_op jit(solution)/shard_map/dot_general | solution.py:78
  179.5 40.0 %psum.42 = f32[3]{0:T(128)S(1)} all-reduce(f32[3]{0:T(128)S(1)} %get-tuple-element.28), channel_id=1, replica_groups=mesh['members'=2,'patch_0'=32,'patch_1'=2,'feat'=4] {'patch_0'}, use_global_device_ids=true, to_apply=%region_4.5 | all-reduce | flops 3 | bytes 24 | tf_op jit(solution)/shard_map/psum | solution.py:18
  219.4 17.1 %psum.43 = f32[3]{0:T(128)S(1)} all-reduce(f32[3]{0:T(128)S(1)} %psum.42), channel_id=1, replica_groups=mesh['members'=2,'patch_0'=32,'patch_1'=2,'feat'=4] {'patch_1'}, use_global_device_ids=true, to_apply=%region_5.6 | all-reduce | flops 3 | bytes 24 | tf_op jit(solution)/shard_map/psum | solution.py:18
  236.7 7.9 %psum.44 = f32[3]{0:T(128)S(1)} all-reduce(f32[3]{0:T(128)S(1)} %psum.43), channel_id=1, replica_groups=mesh['members'=2,'patch_0'=32,'patch_1'=2,'feat'=4] {'feat'}, use_global_device_ids=true, to_apply=%region_6.7 | all-reduce | flops 3 | bytes 24 | tf_op jit(solution)/shard_map/psum | solution.py:18
  248.3 13.4 %all-to-all-start.1 = ((bf16[64,8,512]{2,1,0:T(8,128)(2,1)}), bf16[64,8,512]{2,1,0:T(8,128)(2,1)S(1)}, u32[]{:S(2)}, u32[]{:S(2)}) async-start(bf16[64,8,512]{2,1,0:T(8,128)(2,1)} %bitcast.11), calls=%async_computation.1 | async-start | bytes 1048576 | tf_op jit(solution)/shard_map/all_to_all | solution.py:69
  263.4 61.8 %all-to-all-done.1 = bf16[64,8,512]{2,1,0:T(8,128)(2,1)S(1)} async-done(((bf16[64,8,512]{2,1,0:T(8,128)(2,1)}), bf16[64,8,512]{2,1,0:T(8,128)(2,1)S(1)}, u32[]{:S(2)}, u32[]{:S(2)}) %all-to-all-start.1) | async-done | bytes 524320 | tf_op jit(solution)/shard_map/all_to_all | solution.py:69
  328.0 3.3 gather_fusion.16
  331.3 3.3 gather_fusion.15
  334.6 3.3 gather_fusion.14
  337.9 3.3 gather_fusion.13
  341.3 3.3 gather_fusion.12
  344.6 3.3 gather_fusion.11
  347.9 3.5 gather_fusion.10
  351.5 8.3 %convolution_convert_fusion = bf16[768,512]{1,0:T(8,128)(2,1)} fusion(bf16[768,512]{1,0:T(8,128)(2,1)S(1)} %gather_fusion.17, bf16[768,512]{1,0:T(8,128)(2,1)} %gather_fusion.16, bf16[768,512]{1,0:T(8,128)(2,1)} %gather_fusion.15, bf16[768,512]{1,0:T(8,128)(2,1)} %gather_fusion.14, bf16[768,512]{1,0:T(8,128)(2,1)} %gather_fusion.13, ...), kind=kOutput, calls=%fused_computation.28 | convolution fusion | flops 831258624 | bytes 8921088 | tf_op jit(solution)/shard_map/dot_general | solution.py:78
  359.8 2.9 fusion.57
  363.7 40.0 %psum.45 = f32[3]{0:T(128)S(1)} all-reduce(f32[3]{0:T(128)S(1)} %get-tuple-element.32), channel_id=1, replica_groups=mesh['members'=2,'patch_0'=32,'patch_1'=2,'feat'=4] {'patch_0'}, use_global_device_ids=true, to_apply=%region_10.11 | all-reduce | flops 3 | bytes 24 | tf_op jit(solution)/shard_map/psum | solution.py:18
  403.6 17.1 %psum.46 = f32[3]{0:T(128)S(1)} all-reduce(f32[3]{0:T(128)S(1)} %psum.45), channel_id=1, replica_groups=mesh['members'=2,'patch_0'=32,'patch_1'=2,'feat'=4] {'patch_1'}, use_global_device_ids=true, to_apply=%region_11.12 | all-reduce | flops 3 | bytes 24 | tf_op jit(solution)/shard_map/psum | solution.py:18
  420.8 6.1 %psum.47 = f32[3]{0:T(128)S(1)} all-reduce(f32[3]{0:T(128)S(1)} %psum.46), channel_id=1, replica_groups=mesh['members'=2,'patch_0'=32,'patch_1'=2,'feat'=4] {'feat'}, use_global_device_ids=true, to_apply=%region_12.13 | all-reduce | flops 3 | bytes 24 | tf_op jit(solution)/shard_map/psum | solution.py:18
  (83 shorter events, 30.4 us)
Async XLA Ops:
  7.2 237.4 %copy-start = (f32[3,512]{1,0:T(4,128)S(1)}, f32[3,512]{1,0:T(4,128)}, u32[]{:S(2)}) copy-start(f32[3,512]{1,0:T(4,128)} %param.31) | copy-start | bytes 18436
  20.9 0.8 copy-start.4
  26.1 50.6 %copy-start.1 = (bf16[768,512]{1,0:T(8,128)(2,1)S(1)}, bf16[768,512]{1,0:T(8,128)(2,1)}, u32[]{:S(2)}) copy-start(bf16[768,512]{1,0:T(8,128)(2,1)} %param.16) | copy-start | bytes 2359300
  26.1 51.8 %copy-start.11 = (s32[768,8]{0,1:T(8,128)S(1)}, s32[768,8]{0,1:T(8,128)}, u32[]{:S(2)}) copy-start(s32[768,8]{0,1:T(8,128)} %param.17) | copy-start | bytes 73732
  26.1 52.0 %copy-start.15 = (s32[768]{0:T(1024)S(1)}, s32[768]{0:T(1024)}, u32[]{:S(2)}) copy-start(s32[768]{0:T(1024)} %param.18) | copy-start | bytes 9220
  26.1 52.1 %copy-start.8 = (bf16[1,512,128]{2,1,0:T(8,128)(2,1)S(1)}, bf16[1,512,128]{2,1,0:T(8,128)(2,1)}, u32[]{:S(2)}) copy-start(bf16[1,512,128]{2,1,0:T(8,128)(2,1)} %param.24) | copy-start | bytes 393220
  26.1 113.8 %all-to-all-start = ((bf16[64,8,512]{2,1,0:T(8,128)(2,1)}), bf16[64,8,512]{2,1,0:T(8,128)(2,1)S(1)}, u32[]{:S(2)}, u32[]{:S(2)}) async-start(bf16[64,8,512]{2,1,0:T(8,128)(2,1)} %bitcast.2), calls=%async_computation | async-start | bytes 1048576 | tf_op jit(solution)/shard_map/all_to_all | solution.py:69
  75.9 14.6 %copy-start.9 = (bf16[1,512,128]{2,1,0:T(8,128)(2,1)S(1)}, bf16[1,512,128]{2,1,0:T(8,128)(2,1)}, u32[]{:S(2)}) copy-start(bf16[1,512,128]{2,1,0:T(8,128)(2,1)} %param.26) | copy-start | bytes 393220
  75.9 47.5 %all-gather.2.cloned.1.call-start = ((), (), s32[]{:S(2)}) async-start(), calls=%async_computation.2 | async-start | bytes 1310720 | tf_op jit(solution)/shard_map/all_gather | solution.py:57
  76.7 24.7 %copy-start.10 = (bf16[1,512,128]{2,1,0:T(8,128)(2,1)S(1)}, bf16[1,512,128]{2,1,0:T(8,128)(2,1)}, u32[]{:S(2)}) copy-start(bf16[1,512,128]{2,1,0:T(8,128)(2,1)} %param.28) | copy-start | bytes 393220
  162.6 3.5 copy-start.6
  162.6 3.5 copy-start.18
  177.3 1.1 copy-start.2
  177.3 1.1 copy-start.14
  178.4 0.7 copy-start.12
  178.4 0.7 copy-start.13
  178.4 58.1 %copy-start.16 = (f32[16,3]{0,1:T(4,128)S(1)}, f32[16,3]{0,1:T(4,128)}, u32[]{:S(2)}) copy-start(f32[16,3]{0,1:T(4,128)} %param.22) | copy-start | bytes 580
  178.4 58.1 %copy-start.17 = (s32[3]{0:T(128)S(1)}, s32[3]{0:T(128)}, u32[]{:S(2)}) copy-start(s32[3]{0:T(128)} %param.21) | copy-start | bytes 40
  179.1 65.9 %copy-start.5 = (bf16[1,512,512]{2,1,0:T(8,128)(2,1)S(1)}, bf16[1,512,512]{2,1,0:T(8,128)(2,1)}, u32[]{:S(2)}) copy-start(bf16[1,512,512]{2,1,0:T(8,128)(2,1)} %copy-done.4) | copy-start | bytes 1572868
  245.6 16.0 %copy-start.3 = (bf16[1,1024,512]{2,1,0:T(8,128)(2,1)S(1)}, bf16[1,1024,512]{2,1,0:T(8,128)(2,1)}, u32[]{:S(2)}) copy-start(bf16[1,1024,512]{2,1,0:T(8,128)(2,1)} %all-gather.2.cloned.1.call-done) | copy-start | bytes 3145732
  248.3 76.9 %all-to-all-start.1 = ((bf16[64,8,512]{2,1,0:T(8,128)(2,1)}), bf16[64,8,512]{2,1,0:T(8,128)(2,1)S(1)}, u32[]{:S(2)}, u32[]{:S(2)}) async-start(bf16[64,8,512]{2,1,0:T(8,128)(2,1)} %bitcast.11), calls=%async_computation.1 | async-start | bytes 1048576 | tf_op jit(solution)/shard_map/all_to_all | solution.py:69
  347.9 3.5 copy-start.7
Sparse Core Ops, SparseCore 0:
  78.8 44.5 all-gather.1
where the time goes:
time: 442 us; the launch traced here: 436 us
  blocking collectives  180 us (41%)
  waiting for transfers between devices  81.9 us (19%)
  starting transfers between devices  63.2 us (14%)
  local copies, waits for them, and re-layouts  62.9 us (14%)
  matrix products  30.8 us (7%)
  between operations  14.6 us (3%)
    psum x6, blocking collectives, over_axes(): x = lax.psum(x, axis)  128 us
    all_to_all x2, waiting for transfers between devices, shards(): lax.all_to_all(outgoing, PATCH, split_axis=0, concat_axis=0, tiled=True)  75.4 us
    all_to_all x2, starting transfers between devices, shards(): lax.all_to_all(outgoing, PATCH, split_axis=0, concat_axis=0, tiled=True)  63.2 us
    gather x16, local copies, waits for them, and re-layouts, shards(): edge_value = table[neighbours[:, position]].astype(jnp.float32) + receiver  52.3 us
    dot_general x2, matrix products, shards(): jnp.dot(summed, kept[2][0], preferred_element_type=jnp.float32)  16.6 us
    all_gather x1, blocking collectives, shards(): lax.all_gather(w_out, 'feat', axis=2, tiled=True)  16.3 us
    all_gather x1, blocking collectives, shards(): lax.all_gather(w_send, 'feat', axis=2, tiled=True)  12.8 us
    all_gather x1, blocking collectives, shards(): lax.all_gather(w_recv, 'feat', axis=2, tiled=True)  12.3 us
  transfers between devices with their start and end apart: 3, of which 3 were waited for; matrix products, arithmetic and copies ran while one was open for 1% of the time, Pallas kernels for 0%

commit v1 on v0

v1 whole, which is shorter than its diff:
```python
import functools

import jax
import jax.numpy as jnp
from jax import lax
from jax.experimental import pallas as pl
from jax.experimental.pallas import tpu as pltpu
from jax.sharding import PartitionSpec as P

STEPS = 2
EPSILON = 1e-05
DEAD = -1e30
MESH = pl.DeviceIdType.MESH
F32 = jnp.float32
BF16 = jnp.bfloat16
NT = (((1,), (1,)), ((), ()))


def mm(a, b):
    return jnp.dot(a, b, preferred_element_type=F32)


def half_silu(half):
    return half * jnp.tanh(half) + half


def softplus(x):
    return jnp.maximum(x, 0.0) + jnp.log1p(jnp.exp(-jnp.abs(x)))


def kernel(
    n_patch,
    n_feat,
    h_ref,
    nbr_ref,
    deg_ref,
    rows_ref,
    area_ref,
    scen_ref,
    tot_ref,
    ws_ref,
    wr_ref,
    be_ref,
    wm_ref,
    wn_ref,
    wo_ref,
    gain_ref,
    wd_ref,
    we_ref,
    out_ref,
    cons_ref,
    w,
    ids,
    ohs,
    ohl,
    ohf,
    ohn,
    pre,
    acc,
    table,
    recv_half,
    h_node,
    h_next,
    send,
    recv,
    ar_src,
    ar_all,
    ax_src,
    ax_all,
    wl_sem,
    ws_sem,
    wr_sem,
    fs_sem,
    fr_sem,
    as_sem,
    ar_sem,
    ps_sem,
    pr_sem,
    xs_sem,
    xr_sem,
):
    nodes, width = h_ref.shape
    deg = nbr_ref.shape[0]
    slot = rows_ref.shape[0]
    blocks, block = acc.shape[0], acc.shape[1]
    cols = ws_ref.shape[2]
    half = n_patch // 2
    quarter = n_patch // 4
    fan = half * slot
    pieces = w.shape[0]
    me = lax.axis_index("patch")
    feat = lax.axis_index("feat")
    core = lax.rem(me, 2)
    partner = me + 1 - 2 * core

    def peer(offset):
        return lax.rem(me + offset, n_patch)

    def side(offset):
        return lax.rem(feat + offset, n_feat)

    barrier = pltpu.get_barrier_semaphore()

    def greet(offset, carry):
        pl.semaphore_signal(barrier, inc=1, device_id={"patch": peer(offset)}, device_id_type=MESH)
        return carry

    for offset in range(1, n_feat):
        pl.semaphore_signal(barrier, inc=1, device_id={"feat": side(offset)}, device_id_type=MESH)
    lax.fori_loop(1, n_patch, greet, 0)

    span = width // 2
    mine = pl.ds(pl.multiple_of(core * span, span), span)
    own_cols = pl.ds(pl.multiple_of(feat * cols, cols), cols)
    low = pl.ds(pl.multiple_of(core * span, span), span)
    high = pl.ds(pl.multiple_of(width + core * span, span), span)
    shards = (
        ws_ref.at[0, low],
        wr_ref.at[0, low],
        wn_ref.at[0, low],
        wm_ref.at[0, low],
        wn_ref.at[0, high],
        wo_ref.at[0, low],
    )
    local = [
        pltpu.make_async_copy(shards[i], w.at[i, mine, own_cols], wl_sem.at[i])
        for i in range(pieces)
    ]
    for copy in local:
        copy.start()

    picks = rows_ref[...].T.astype(F32)
    total_rows = n_patch * slot
    spread = jnp.where(
        lax.broadcasted_iota(jnp.int32, (total_rows, n_patch), 0) // slot
        == lax.broadcasted_iota(jnp.int32, (total_rows, n_patch), 1),
        1.0,
        0.0,
    ).astype(BF16)
    coarse = jnp.floor(picks * (1.0 / 16.0))
    fine = picks - 16.0 * coarse
    each = mm(spread, coarse.astype(BF16)) * 16.0 + mm(spread, fine.astype(BF16))
    lane = lax.broadcasted_iota(jnp.int32, (total_rows, slot), 1)
    turn = lax.broadcasted_iota(jnp.int32, (total_rows, slot), 0) % slot
    chosen_row = jnp.sum(jnp.where(lane == turn, each, 0.0), axis=1, keepdims=True)
    node_at = lax.broadcasted_iota(jnp.int32, (total_rows, nodes), 1).astype(F32)
    ohs[...] = jnp.where(chosen_row == node_at, 1.0, 0.0).astype(BF16)

    def fill_send(step, source):
        picked = mm(ohs[...], source).astype(BF16).reshape(n_patch, slot, width)
        send[step] = picked
        recv[step, pl.ds(quarter, 1)] = send[step, pl.ds(me, 1)]

    fill_send(0, h_ref[...])

    pl.semaphore_wait(barrier, n_patch - 1 + n_feat - 1)

    def exchange(step, offset, group):
        target = peer(offset)
        place = lax.rem(n_patch - offset + quarter, n_patch)
        pltpu.make_async_remote_copy(
            src_ref=send.at[step, target],
            dst_ref=recv.at[step, place],
            send_sem=as_sem.at[step],
            recv_sem=ar_sem.at[step, group],
            device_id={"patch": target},
            device_id_type=MESH,
        ).start()

    def start_exchange(step):
        def pair(group):
            def body(j, carry):
                exchange(step, half - j, group)
                exchange(step, half + j, group)
                return carry

            return body

        exchange(step, half, 1)
        lax.fori_loop(1, quarter, pair(1), 0)
        exchange(step, half + quarter, 1)
        exchange(step, quarter, 0)
        lax.fori_loop(quarter + 1, half, pair(0), 0)

    def wait_far(step):
        ref = recv.at[step, pl.ds(half, half)]
        pltpu.make_async_copy(ref, ref, ar_sem.at[step, 1]).wait()

    def wait_near(step):
        ref = recv.at[step, pl.ds(0, half - 1)]
        pltpu.make_async_copy(ref, ref, ar_sem.at[step, 0]).wait()

    start_exchange(0)

    def shard_copy(i, offset):
        return pltpu.make_async_remote_copy(
            src_ref=w.at[i, mine, own_cols],
            dst_ref=w.at[i, mine, own_cols],
            send_sem=ws_sem.at[i, offset - 1],
            recv_sem=wr_sem.at[i, offset - 1],
            device_id={"feat": side(offset)},
            device_id_type=MESH,
        )

    for i in range(pieces):
        local[i].wait()
        for offset in range(1, n_feat):
            shard_copy(i, offset).start()

    def swap_copy(i):
        return pltpu.make_async_remote_copy(
            src_ref=w.at[i, mine],
            dst_ref=w.at[i, mine],
            send_sem=fs_sem.at[i],
            recv_sem=fr_sem.at[i],
            device_id={"patch": partner},
            device_id_type=MESH,
        )

    def pass_on(i):
        for offset in range(1, n_feat):
            shard_copy(i, offset).wait_recv()
        swap_copy(i).start()

    raw = nbr_ref[...]
    far_id = jnp.maximum(raw - nodes, 0)
    place = far_id // slot - me + quarter
    place = jnp.where(place < 0, place + n_patch, place)
    place = jnp.where(place >= n_patch, place - n_patch, place)
    ordered = jnp.where(raw < nodes, raw, nodes + place * slot + far_id % slot)
    live = lax.broadcasted_iota(jnp.int32, raw.shape, 0) < deg_ref[...]
    ids[...] = jnp.where(live, ordered, -1).T

    def select(b, carry):
        rows = pl.ds(b * block, block)
        mine_ids = ids[rows]
        for k in range(deg):
            col = mine_ids[:, k : k + 1]
            at = b * deg + k
            for ref, base in ((ohl, 0), (ohn, nodes), (ohf, nodes + fan)):
                here = lax.broadcasted_iota(jnp.int32, ref.shape[1:], 1) + base
                ref[at] = jnp.where(col == here, 1.0, 0.0).astype(BF16)
        return carry

    lax.fori_loop(0, blocks, select, 0)

    fields = wd_ref.shape[0]
    nodes_all = float(nodes * n_patch * n_feat)
    scenario_at = lax.broadcasted_iota(jnp.int32, tot_ref.shape, 0)
    target = jnp.sum(jnp.where(scenario_at == scen_ref[...], tot_ref[...], 0.0), axis=0, keepdims=True)
    diagonal = lax.broadcasted_iota(jnp.int32, (fields, fields), 0) == lax.broadcasted_iota(
        jnp.int32, (fields, fields), 1
    )
    lanes = ar_src.shape[2]

    def start_sum(step, local_fields):
        part = jnp.sum(local_fields * area_ref[...], axis=1, keepdims=True)
        wide = jnp.broadcast_to(part, (fields, lanes))
        mark = lax.broadcasted_iota(jnp.int32, (fields, lanes), 0) == lax.broadcasted_iota(
            jnp.int32, (fields, lanes), 1
        )
        line = jnp.sum(jnp.where(mark, wide, 0.0), axis=0, keepdims=True)
        ar_src[step] = line
        ar_all[step, pl.ds(me, 1)] = line.reshape(1, 1, lanes)

        def one(offset):
            pltpu.make_async_remote_copy(
                src_ref=ar_src.at[step],
                dst_ref=ar_all.at[step, me],
                send_sem=ps_sem.at[step],
                recv_sem=pr_sem.at[step],
                device_id={"patch": peer(offset)},
                device_id_type=MESH,
            ).start()

        def both(j, carry):
            one(half - j)
            one(half + j)
            return carry

        one(half)
        lax.fori_loop(1, half, both, 0)

    def side_copy(step, offset):
        return pltpu.make_async_remote_copy(
            src_ref=ax_src.at[step],
            dst_ref=ax_all.at[step, feat],
            send_sem=xs_sem.at[step, offset - 1],
            recv_sem=xr_sem.at[step, offset - 1],
            device_id={"feat": side(offset)},
            device_id_type=MESH,
        )

    def finish_sum(step):
        ref = ar_all.at[step, pl.ds(0, n_patch - 1)]
        pltpu.make_async_copy(ref, ref, pr_sem.at[step]).wait()
        line = jnp.sum(ar_all[step], axis=0)
        ax_src[step] = line
        ax_all[step, pl.ds(feat, 1)] = line.reshape(1, 1, lanes)
        for offset in range(1, n_feat):
            side_copy(step, offset).start()
        for offset in range(1, n_feat):
            side_copy(step, offset).wait_recv()
        integral = jnp.sum(ax_all[step], axis=0)[:, :fields]
        scale = target * nodes_all / integral
        wide = jnp.broadcast_to(scale, (fields, fields))
        return jnp.sum(jnp.where(diagonal, wide, 0.0), axis=1, keepdims=True)

    wd = wd_ref[...]

    def rescaled(rows, mix):
        part = softplus(lax.dot_general(rows, wd, NT, preferred_element_type=F32))
        change = jnp.dot(part, mix, precision=lax.Precision.HIGHEST, preferred_element_type=F32)
        return (rows.astype(F32) + change).astype(BF16)

    def project(b, carry):
        rows = pl.ds(b * block, block)
        latent = h_next[rows]
        table[rows] = (0.5 * mm(latent, w[0])).astype(BF16)
        recv_half[b] = 0.5 * (mm(latent, w[1]) + be_ref[...])
        return carry

    def local_edges(b, carry):
        mine_ids = ids[pl.ds(b * block, block)]
        base = recv_half[b]
        for k in range(deg):
            dead = jnp.where(mine_ids[:, k : k + 1] < 0, DEAD, 0.0)
            at = b * deg + k
            pre[at] = mm(ohl[at], table[pl.ds(0, nodes)]) + (base + dead)
        return carry

    def node_part(b, carry):
        h_node[b] = mm(h_next[pl.ds(b * block, block)], w[2])
        return carry

    def far_edges(i, carry):
        pre[i] += mm(ohf[i], table[pl.ds(nodes + fan, fan)])
        return carry

    def finish_block(b, carry):
        total = jnp.zeros((block, width), F32)
        for k in range(deg):
            at = b * deg + k
            total = total + half_silu(pre[at] + mm(ohn[at], table[pl.ds(nodes, fan)]))
        message = mm(total.astype(BF16), w[3]).astype(BF16)
        hidden = half_silu(0.5 * (h_node[b] + mm(message, w[4]))).astype(BF16)
        output = mm(hidden, w[5])
        average = jnp.mean(output, axis=1, keepdims=True)
        centred = output - average
        variance = jnp.mean(jnp.square(centred), axis=1, keepdims=True)
        normed = centred * lax.rsqrt(variance + EPSILON) * gain_ref[...]
        rows = pl.ds(b * block, block)
        h_next[rows] = (h_next[rows].astype(F32) + normed).astype(BF16)
        return carry

    def received(step, base, count):
        return recv[step, pl.ds(base, count)].reshape(count * slot, width)

    h_next[...] = h_ref[...]
    pass_on(0)
    pass_on(1)
    swap_copy(0).wait_recv()
    swap_copy(1).wait_recv()
    lax.fori_loop(0, blocks, project, 0)
    lax.fori_loop(0, blocks, local_edges, 0)
    for i in range(2, pieces):
        pass_on(i)
    for i in range(2, pieces):
        swap_copy(i).wait_recv()
    lax.fori_loop(0, blocks, node_part, 0)

    scale = None
    for step in range(STEPS):
        if step > 0:
            scale = finish_sum(step - 1)
            cons_ref[step - 1] = scale * local_fields
            mix = (scale - 1.0) * we_ref[...]

            def move(b, carry):
                rows = pl.ds(b * block, block)
                h_next[rows] = rescaled(h_next[rows], mix)
                return carry

            lax.fori_loop(0, blocks, move, 0)
            lax.fori_loop(0, blocks, project, 0)
            lax.fori_loop(0, blocks, local_edges, 0)
            lax.fori_loop(0, blocks, node_part, 0)

        def place_rows(base):
            rows = received(step, base, half)
            if step > 0:
                rows = rescaled(rows, mix)
            table[pl.ds(nodes + base * slot, fan)] = (0.5 * mm(rows, w[0])).astype(BF16)

        wait_far(step)
        place_rows(half)
        lax.fori_loop(0, blocks * deg, far_edges, 0)
        wait_near(step)
        place_rows(0)
        lax.fori_loop(0, blocks, finish_block, 0)

        if step + 1 < STEPS:
            fill_send(step + 1, h_next[...])
        local_fields = softplus(lax.dot_general(wd, h_next[...], NT, preferred_element_type=F32))
        start_sum(step, local_fields)
        if step + 1 < STEPS:
            start_exchange(step + 1)

    scale = finish_sum(STEPS - 1)
    cons_ref[STEPS - 1] = scale * local_fields
    mix = (scale - 1.0) * we_ref[...]

    def leave(b, carry):
        rows = pl.ds(b * block, block)
        out_ref[rows] = rescaled(h_next[rows], mix)
        return carry

    lax.fori_loop(0, blocks, leave, 0)

    for i in range(pieces):
        for offset in range(1, n_feat):
            shard_copy(i, offset).wait_send()
        swap_copy(i).wait_send()
    for step in range(STEPS):
        ref = send.at[step, pl.ds(0, n_patch - 1)]
        pltpu.make_async_copy(ref, ref, as_sem.at[step]).wait()
        ref = ar_all.at[step, pl.ds(0, n_patch - 1)]
        pltpu.make_async_copy(ref, ref, ps_sem.at[step]).wait()
        for offset in range(1, n_feat):
            side_copy(step, offset).wait_send()


def shards(
    n_patch,
    n_feat,
    latents,
    neighbours,
    degree,
    send_rows,
    area,
    scenario,
    totals,
    w_send,
    w_recv,
    b_edge,
    w_msg,
    w_node,
    w_out,
    gain,
    w_dec,
    w_enc,
):
    nodes, width = latents.shape
    deg, slot = neighbours.shape[1], send_rows.shape[1]
    fields = w_dec.shape[0]
    block = min(256, nodes)
    blocks = nodes // block
    fan = n_patch // 2 * slot
    pieces = 6
    lanes = 128
    vmem = pl.BlockSpec(memory_space=pltpu.VMEM)
    hbm = pl.BlockSpec(memory_space=pltpu.HBM)
    dma = pltpu.SemaphoreType.DMA
    return pl.pallas_call(
        functools.partial(kernel, n_patch, n_feat),
        out_shape=(
            jax.ShapeDtypeStruct((nodes, width), BF16),
            jax.ShapeDtypeStruct((STEPS, fields, nodes), F32),
        ),
        in_specs=[vmem] * 7 + [hbm, hbm, vmem, hbm, hbm, hbm, vmem, vmem, vmem],
        out_specs=(vmem, vmem),
        scratch_shapes=[
            pltpu.VMEM((pieces, width, width), BF16),
            pltpu.VMEM((nodes, deg), jnp.int32),
            pltpu.VMEM((n_patch * slot, nodes), BF16),
            pltpu.VMEM((blocks * deg, block, nodes), BF16),
            pltpu.VMEM((blocks * deg, block, fan), BF16),
            pltpu.VMEM((blocks * deg, block, fan), BF16),
            pltpu.VMEM((blocks * deg, block, width), F32),
            pltpu.VMEM((blocks, block, width), F32),
            pltpu.VMEM((nodes + 2 * fan, width), BF16),
            pltpu.VMEM((blocks, block, width), F32),
            pltpu.VMEM((blocks, block, width), F32),
            pltpu.VMEM((nodes, width), BF16),
            pltpu.VMEM((STEPS, n_patch, slot, width), BF16),
            pltpu.VMEM((STEPS, n_patch, slot, width), BF16),
            pltpu.VMEM((STEPS, 1, lanes), F32),
            pltpu.VMEM((STEPS, n_patch, 1, lanes), F32),
            pltpu.VMEM((STEPS, 1, lanes), F32),
            pltpu.VMEM((STEPS, n_feat, 1, lanes), F32),
            dma((pieces,)),
            dma((pieces, n_feat - 1)),
            dma((pieces, n_feat - 1)),
            dma((pieces,)),
            dma((pieces,)),
            dma((STEPS,)),
            dma((STEPS, 2)),
            dma((STEPS,)),
            dma((STEPS,)),
            dma((STEPS, n_feat - 1)),
            dma((STEPS, n_feat - 1)),
        ],
        compiler_params=pltpu.CompilerParams(
            collective_id=0, has_side_effects=True, vmem_limit_bytes=63 * 1024 * 1024
        ),
    )(
        latents,
        neighbours.T,
        degree[None, :],
        send_rows.T,
        area[None, :],
        scenario[None, :],
        totals,
        w_send,
        w_recv,
        b_edge,
        w_msg,
        w_node,
        w_out,
        gain,
        w_dec,
        w_enc,
    )


def solution(mesh):
    every = ("members", "patch", "feat")
    group = ("patch", "feat")
    column = P(None, None, "feat")
    return jax.shard_map(
        functools.partial(shards, mesh.shape["patch"], mesh.shape["feat"]),
        mesh=mesh,
        in_specs=(
            P(every, None),
            P(group, None),
            P(group),
            P(group, None),
            P(group),
            P("members"),
            P(),
            column,
            column,
            P(),
            column,
            column,
            column,
            P(),
            P(),
            P(),
        ),
        out_specs=(P(every, None), P("members", None, group)),
        check_vma=False,
    )
```

time: 442 us -> 195 us (0.44); the launches traced: 436 us -> 195 us
  Pallas kernels: 0 us -> 188 us
  blocking collectives: 180 us -> 0 us
  waiting for transfers between devices: 81.9 us -> 0 us
  starting transfers between devices: 63.2 us -> 0 us
  local copies, waits for them, and re-layouts: 62.9 us -> 6.03 us
  matrix products: 30.8 us -> 0 us
  between operations: 14.6 us -> 0.66 us
    pallas_call x0 -> x1, Pallas kernels: none -> 188 us  [shards(): pl.pallas_call(functools.partial(kernel, n_patch, n_feat), out_shape=(jax...]
    psum x6 -> x0, blocking collectives: 128 us -> none  [over_axes(): x = lax.psum(x, axis)]
    all_to_all x2 -> x0, waiting for transfers between devices: 75.4 us -> none  [shards(): lax.all_to_all(outgoing, PATCH, split_axis=0, concat_axis=0, tiled=True)]
    all_to_all x2 -> x0, starting transfers between devices: 63.2 us -> none  [shards(): lax.all_to_all(outgoing, PATCH, split_axis=0, concat_axis=0, tiled=True)]
    gather x18 -> x0, local copies, waits for them, and re-layouts: 57.5 us -> none  [the longest x16 52.3 us: shards(): edge_value = table[neighbours[:, position]].astype(jnp.float32) + receiver]
    all_gather x4 -> x0, blocking collectives: 52.4 us -> none  [the longest x1 16.3 us: shards(): lax.all_gather(w_out, 'feat', axis=2, tiled=True)]
    dot_general x12 -> x0, matrix products: 30.8 us -> none  [the longest x2 16.6 us: shards(): jnp.dot(summed, kept[2][0], preferred_element_type=jnp.float32)]
    all_gather x1 -> x0, waiting for transfers between devices: 5.75 us -> none  [shards(): lax.all_gather(w_node, 'feat', axis=2, tiled=True)]
  transfers between devices with their start and end apart: 3 -> 0, of which waited for: 3 -> 0; matrix products, arithmetic and copies ran while one was open for 1% -> 0% of each run, Pallas kernels for 0% -> 0%
where the time goes in v1:
time: 195 us
  Pallas kernels  188 us (96%)
  local copies, waits for them, and re-layouts  6.03 us (3%)
    pallas_call x1, Pallas kernels, shards(): pl.pallas_call(functools.partial(kernel, n_patch, n_feat), out_shape=(jax...  188 us

profile of v1, /device:TPU:33, one launch (start us, length us, event | category | flops | bytes accessed | tf_op | source)
XLA Modules:
  0.0 194.9 jit_solution(14431199387663081547)
XLA Ops:
  0.6 0.0 copy-start
  0.6 0.0 copy-start.1
  0.6 0.7 copy-done
  1.3 0.6 broadcast_in_dim.9.deg_ref
  1.9 0.0 copy-done.1
  1.9 0.0 copy-start.2
  1.9 0.6 broadcast_in_dim.10.area_ref
  2.5 0.1 copy-done.2
  2.6 0.7 copy.18.tot_ref
  3.3 188.2 %shard_map.167 = (bf16[768,512]{1,0:T(8,128)(2,1)}, f32[2,3,768]{2,1,0:T(4,128)}) custom-call(bf16[768,512]{1,0:T(8,128)(2,1)} %h_ref.1, s32[8,768]{1,0:T(8,128)} %bitcast.3, s32[1,768]{1,0:T(1,128)} %broadcast_in_dim.9.deg_ref, s32[8,64]{1,0:T(8,128)} %bitcast.4, f32[1,768]{1,0:T(1,128)} %broadcast_in_dim.10.area_ref, s32[1,3]{1,0:T(1,128)} %bitcast.5, ...), custom_call_target="tpu_custom_call" | custom-call | tf_op jit(solution)/shard_map/pallas_call | solution.py:464
  191.5 1.4 copy.19
  192.9 2.1 %copy.21 = bf16[768,512]{1,0:T(8,128)(2,1)} copy(bf16[768,512]{1,0:T(8,128)(2,1)} %get-tuple-element.6) | data formatting | bytes 1572864
Async XLA Ops:
  0.6 0.7 copy-start
  0.6 1.3 copy-start.1
  1.9 0.7 copy-start.2

commit v2 on v1

v2 whole, which is shorter than its diff:
```python
import functools

import jax
import jax.numpy as jnp
from jax import lax
from jax.experimental import pallas as pl
from jax.experimental.pallas import tpu as pltpu
from jax.sharding import PartitionSpec as P

STEPS = 2
EPSILON = 1e-05
DEAD = -1e30
MESH = pl.DeviceIdType.MESH
F32 = jnp.float32
BF16 = jnp.bfloat16
NT = (((1,), (1,)), ((), ()))


def mm(a, b):
    return jnp.dot(a, b, preferred_element_type=F32)


def half_silu(half):
    return half * jnp.tanh(half) + half


def softplus(x):
    return jnp.maximum(x, 0.0) + jnp.log1p(jnp.exp(-jnp.abs(x)))


def kernel(
    n_patch,
    n_feat,
    h_ref,
    nbr_ref,
    deg_ref,
    rows_ref,
    area_ref,
    scen_ref,
    tot_ref,
    ws_ref,
    wr_ref,
    be_ref,
    wm_ref,
    wn_ref,
    wo_ref,
    gain_ref,
    wd_ref,
    we_ref,
    out_ref,
    cons_ref,
    w,
    ids,
    ohs,
    ohl,
    ohr,
    pre,
    table,
    recv_half,
    h_node,
    h_next,
    summed,
    send,
    recv,
    ar_src,
    ar_all,
    ax_src,
    ax_all,
    in_sem,
    token_sem,
    h_sem,
    wl_sem,
    ws_sem,
    wr_sem,
    fs_sem,
    fr_sem,
    as_sem,
    ar_sem,
    ps_sem,
    pr_sem,
    xs_sem,
    xr_sem,
):
    nodes, width = h_ref.shape
    deg = nbr_ref.shape[0]
    slot = rows_ref.shape[0]
    groups, packed = pre.shape[0], pre.shape[1]
    few = packed // deg
    blocks, block = h_node.shape[0], h_node.shape[1]
    cols = ws_ref.shape[2]
    half = n_patch // 2
    parts = ar_sem.shape[1]
    part_slots = n_patch // parts
    remote = n_patch * slot
    pieces = w.shape[0]
    unroll = 4 if groups % 4 == 0 else 1
    me = lax.axis_index("patch")
    feat = lax.axis_index("feat")
    core = lax.rem(me, 2)
    partner = me + 1 - 2 * core

    def peer(offset):
        return lax.rem(me + offset, n_patch)

    def side(offset):
        return lax.rem(feat + offset, n_feat)

    rank = lax.rem(me + n_patch - 1, n_patch)
    ahead = peer(1)
    behind = peer(n_patch - 1)
    barrier = pltpu.get_barrier_semaphore()
    pl.semaphore_signal(barrier, inc=1, device_id={"patch": behind}, device_id_type=MESH)
    for offset in range(1, n_feat):
        pl.semaphore_signal(barrier, inc=1, device_id={"feat": side(offset)}, device_id_type=MESH)

    span = width // 2
    mine = pl.ds(pl.multiple_of(core * span, span), span)
    low = mine
    high = pl.ds(pl.multiple_of(width + core * span, span), span)
    shards = (
        ws_ref.at[0, low],
        wr_ref.at[0, low],
        wn_ref.at[0, low],
        wm_ref.at[0, low],
        wn_ref.at[0, high],
        wo_ref.at[0, low],
    )

    def cols_of(owner):
        return pl.ds(pl.multiple_of(owner * cols, cols), cols)

    own_cols = cols_of(feat)
    load_h = pltpu.make_async_copy(h_ref, h_next, h_sem)
    local = [
        pltpu.make_async_copy(shards[i], w.at[i, mine, own_cols], wl_sem.at[i])
        for i in range(pieces)
    ]
    local[0].start()
    local[1].start()
    load_h.start()
    for i in range(2, pieces):
        local[i].start()

    pl.semaphore_wait(barrier, n_feat)

    @pl.when(rank > 0)
    def _():
        pl.semaphore_wait(token_sem, 1)

    @pl.when(rank < n_patch - 1)
    def _():
        pl.semaphore_signal(token_sem, inc=1, device_id={"patch": ahead}, device_id_type=MESH)

    def arrive(back, carry):
        pl.semaphore_signal(
            in_sem.at[rank],
            inc=1,
            device_id={"patch": peer(n_patch - back)},
            device_id_type=MESH,
        )
        return carry

    lax.fori_loop(1, rank + 1, arrive, 0)

    def side_part(i, rows, owner, to, at):
        ref = w.at[i, rows, cols_of(owner)]
        return pltpu.make_async_remote_copy(
            src_ref=ref,
            dst_ref=ref,
            send_sem=ws_sem.at[i, at],
            recv_sem=wr_sem.at[i, at],
            device_id={"feat": to},
            device_id_type=MESH,
        )

    right, left = side(1), side(n_feat - 1)
    relay = n_feat == 4
    quart = span // 2
    rows_a = pl.ds(pl.multiple_of(core * span, quart), quart)
    rows_b = pl.ds(pl.multiple_of(core * span + quart, quart), quart)

    def first_copies(i):
        if relay:
            return [side_part(i, mine, feat, right, 0), side_part(i, mine, feat, left, 1)]
        return [side_part(i, mine, feat, side(o), o - 1) for o in range(1, n_feat)]

    def relay_copies(i):
        if relay:
            return [side_part(i, rows_a, left, right, 2), side_part(i, rows_b, right, left, 3)]
        return []

    def swap_copy(i):
        return pltpu.make_async_remote_copy(
            src_ref=w.at[i, mine],
            dst_ref=w.at[i, mine],
            send_sem=fs_sem.at[i],
            recv_sem=fr_sem.at[i],
            device_id={"patch": partner},
            device_id_type=MESH,
        )

    def own_out(i):
        local[i].wait()
        for copy in first_copies(i):
            copy.start()

    def pass_on(i):
        for copy in first_copies(i):
            copy.wait_recv()
        for copy in relay_copies(i):
            copy.start()

    def pass_over(i):
        for copy in relay_copies(i):
            copy.wait_recv()
        swap_copy(i).start()

    own_out(0)
    own_out(1)

    picks = rows_ref[...].T.astype(F32)
    spread = jnp.where(
        lax.broadcasted_iota(jnp.int32, (remote, n_patch), 0) // slot
        == lax.broadcasted_iota(jnp.int32, (remote, n_patch), 1),
        1.0,
        0.0,
    ).astype(BF16)
    coarse = jnp.floor(picks * (1.0 / 16.0))
    fine = picks - 16.0 * coarse
    each = mm(spread, coarse.astype(BF16)) * 16.0 + mm(spread, fine.astype(BF16))
    lane = lax.broadcasted_iota(jnp.int32, (remote, slot), 1)
    turn = lax.broadcasted_iota(jnp.int32, (remote, slot), 0) % slot
    chosen_row = jnp.sum(jnp.where(lane == turn, each, 0.0), axis=1, keepdims=True)
    node_at = lax.broadcasted_iota(jnp.int32, (remote, nodes), 1).astype(F32)
    ohs[...] = jnp.where(chosen_row == node_at, 1.0, 0.0).astype(BF16)

    def fill_send(step):
        picked = mm(ohs[...], h_next[...]).astype(BF16).reshape(n_patch, slot, width)
        send[step] = picked
        recv[step, pl.ds(n_patch - 1, 1)] = send[step, pl.ds(me, 1)]

    load_h.wait()
    fill_send(0)

    def slot_of(d):
        return jnp.where(d < 0, -2 * d - 1, 2 * d)

    def exchange(step, offset):
        target = peer(offset)
        place = slot_of(half - offset)
        pltpu.make_async_remote_copy(
            src_ref=send.at[step, target],
            dst_ref=recv.at[step, place],
            send_sem=as_sem.at[step],
            recv_sem=ar_sem.at[step, place // part_slots],
            device_id={"patch": target},
            device_id_type=MESH,
        ).start()

    def exchange_pairs(step, first, last):
        def body(j, carry):
            exchange(step, half - j)
            exchange(step, half + j)
            return carry

        if first == 0:
            exchange(step, half)
        lax.fori_loop(max(first, 1), last, body, 0)

    def wait_part(step, g):
        count = part_slots - 1 if g == parts - 1 else part_slots
        ref = recv.at[step, pl.ds(0, count)]
        pltpu.make_async_copy(ref, ref, ar_sem.at[step, g]).wait()

    def send_back(back, carry):
        exchange(0, n_patch - back)
        return carry

    def send_ahead(on, carry):
        pl.semaphore_wait(in_sem.at[rank + on], 1)
        exchange(0, on)
        return carry

    lax.fori_loop(1, rank + 1, send_back, 0)
    pass_on(0)
    pass_on(1)
    for i in range(2, pieces):
        own_out(i)
    lax.fori_loop(1, n_patch - rank, send_ahead, 0)

    raw = nbr_ref[...]
    far_id = jnp.maximum(raw - nodes, 0)
    source = far_id // slot - me
    source = jnp.where(source < 0, source + n_patch, source)
    ordered = jnp.where(raw < nodes, raw, nodes + slot_of(source - half) * slot + far_id % slot)
    live = lax.broadcasted_iota(jnp.int32, raw.shape, 0) < deg_ref[...].reshape(1, nodes)
    ids[...] = jnp.where(live, ordered, -1).T

    def select(g, carry):
        mine_ids = ids[pl.ds(g * few, few)]
        for k in range(deg):
            col = mine_ids[:, k : k + 1]
            for ref, base in ((ohl, 0), (ohr, nodes)):
                here = lax.broadcasted_iota(jnp.int32, (few, ref.shape[2]), 1) + base
                ref[g, pl.ds(k * few, few)] = jnp.where(col == here, 1.0, 0.0).astype(BF16)
        return carry

    lax.fori_loop(0, groups, select, 0)

    fields = wd_ref.shape[0]
    nodes_all = float(nodes * n_patch * n_feat)
    field_at = lax.broadcasted_iota(jnp.int32, tot_ref.shape, 0)
    wanted = jnp.zeros(tot_ref.shape, jnp.int32)
    for f in range(fields):
        wanted = jnp.where(field_at == f, scen_ref[f], wanted)
    scenario_at = lax.broadcasted_iota(jnp.int32, tot_ref.shape, 1)
    target = jnp.sum(jnp.where(scenario_at == wanted, tot_ref[...], 0.0), axis=1, keepdims=True)
    lanes = ar_src.shape[2]
    mark = lax.broadcasted_iota(jnp.int32, (fields, lanes), 0) == lax.broadcasted_iota(
        jnp.int32, (fields, lanes), 1
    )
    plane = 2 * n_feat
    seat = core * n_feat + feat
    depth = lax.div(me, 2)

    def seat_copy(step, offset):
        other = lax.rem(seat + offset, plane)
        other_core = lax.div(other, n_feat)
        return pltpu.make_async_remote_copy(
            src_ref=ax_src.at[step],
            dst_ref=ax_all.at[step, seat],
            send_sem=xs_sem.at[step],
            recv_sem=xr_sem.at[step],
            device_id={"patch": me - core + other_core, "feat": lax.rem(other, n_feat)},
            device_id_type=MESH,
        )

    def wait_bytes(ref, sem):
        pltpu.make_async_copy(ref, ref, sem).wait()

    def start_sum(step, local_fields):
        area = area_ref[...].reshape(1, nodes)
        part = jnp.sum(local_fields * area, axis=1, keepdims=True)
        wide = jnp.broadcast_to(part, (fields, lanes))
        line = jnp.sum(jnp.where(mark, wide, 0.0), axis=0, keepdims=True)
        ax_src[step] = line
        ax_all[step, pl.ds(seat, 1)] = line.reshape(1, 1, lanes)
        for offset in range(1, plane):
            seat_copy(step, offset).start()
        wait_bytes(ax_all.at[step, pl.ds(0, plane - 1)], xr_sem.at[step])
        line = jnp.sum(ax_all[step], axis=0)
        ar_src[step] = line
        ar_all[step, pl.ds(depth, 1)] = line.reshape(1, 1, lanes)

        def one(offset):
            pltpu.make_async_remote_copy(
                src_ref=ar_src.at[step],
                dst_ref=ar_all.at[step, depth],
                send_sem=ps_sem.at[step],
                recv_sem=pr_sem.at[step],
                device_id={"patch": peer(2 * offset)},
                device_id_type=MESH,
            ).start()

        middle = half // 2

        def both(j, carry):
            one(middle - j)
            one(middle + j)
            return carry

        one(middle)
        lax.fori_loop(1, middle, both, 0)

    def finish_sum(step):
        wait_bytes(ar_all.at[step, pl.ds(0, half - 1)], pr_sem.at[step])
        line = jnp.sum(ar_all[step], axis=0)
        wide = jnp.broadcast_to(line, (fields, lanes))
        integral = jnp.sum(jnp.where(mark, wide, 0.0), axis=1, keepdims=True)
        return target * nodes_all / integral

    wd = wd_ref[...]

    def rescaled(rows, mix):
        part = softplus(lax.dot_general(rows, wd, NT, preferred_element_type=F32))
        change = jnp.dot(part, mix, precision=lax.Precision.HIGHEST, preferred_element_type=F32)
        return (rows.astype(F32) + change).astype(BF16)

    def project(b, carry):
        rows = pl.ds(b * block, block)
        latent = h_next[rows]
        table[rows] = (0.5 * mm(latent, w[0])).astype(BF16)
        recv_half[rows] = 0.5 * (mm(latent, w[1]) + be_ref[...])
        return carry

    def local_edges(t, carry):
        for u in range(unroll):
            g = t * unroll + u
            here = pl.ds(g * few, few)
            mine_ids = ids[here]
            base = recv_half[here]
            found = mm(ohl[g], table[pl.ds(0, nodes)])
            for k in range(deg):
                dead = jnp.where(mine_ids[:, k : k + 1] < 0, DEAD, 0.0)
                pre[g, pl.ds(k * few, few)] = found[k * few : (k + 1) * few] + (base + dead)
        return carry

    def node_part(b, carry):
        h_node[b] = mm(h_next[pl.ds(b * block, block)], w[2])
        return carry

    def remote_edges(t, carry):
        for u in range(unroll):
            g = t * unroll + u
            found = mm(ohr[g], table[pl.ds(nodes, remote)])
            total = jnp.zeros((few, width), F32)
            for k in range(deg):
                rows = pl.ds(k * few, few)
                total = total + half_silu(pre[g, rows] + found[k * few : (k + 1) * few])
            summed[pl.ds(g * few, few)] = total.astype(BF16)
        return carry

    def finish_block(b):
        rows = pl.ds(b * block, block)
        message = mm(summed[rows], w[3]).astype(BF16)
        hidden = half_silu(0.5 * (h_node[b] + mm(message, w[4]))).astype(BF16)
        output = mm(hidden, w[5])
        average = jnp.mean(output, axis=1, keepdims=True)
        centred = output - average
        variance = jnp.mean(jnp.square(centred), axis=1, keepdims=True)
        normed = centred * lax.rsqrt(variance + EPSILON) * gain_ref[...]
        h_next[rows] = (h_next[rows].astype(F32) + normed).astype(BF16)

    def place_part(step, g, mix):
        rows = recv[step, pl.ds(g * part_slots, part_slots)]
        rows = rows.reshape(part_slots * slot, width)
        if step > 0:
            rows = rescaled(rows, mix)
        at = pl.ds(nodes + g * part_slots * slot, part_slots * slot)
        table[at] = (0.5 * mm(rows, w[0])).astype(BF16)

    pass_over(0)
    pass_over(1)
    swap_copy(0).wait_recv()
    swap_copy(1).wait_recv()
    lax.fori_loop(0, blocks, project, 0)
    for i in range(2, pieces):
        pass_on(i)
    lax.fori_loop(0, groups // unroll, local_edges, 0)
    for i in range(2, pieces):
        pass_over(i)

    mix = None
    for step in range(STEPS):
        if step > 0:
            scale = finish_sum(step - 1)
            for f in range(fields):
                cons_ref[f, step - 1 : step] = (scale * local_fields)[f : f + 1]
            mix = (scale - 1.0) * we_ref[...]

            def move(b, carry):
                rows = pl.ds(b * block, block)
                h_next[rows] = rescaled(h_next[rows], mix)
                return carry

            lax.fori_loop(0, blocks, move, 0)
            lax.fori_loop(0, blocks, project, 0)
            lax.fori_loop(0, groups // unroll, local_edges, 0)
            lax.fori_loop(0, blocks, node_part, 0)

        for g in range(parts):
            wait_part(step, g)
            place_part(step, g, mix)
        lax.fori_loop(0, groups // unroll, remote_edges, 0)
        if step == 0:
            for i in range(2, pieces):
                swap_copy(i).wait_recv()
            lax.fori_loop(0, blocks, node_part, 0)
        for b in range(blocks):
            finish_block(b)

        if step + 1 < STEPS:
            fill_send(step + 1)
            early = half // 4
            exchange_pairs(step + 1, 0, early)
        local_fields = softplus(lax.dot_general(wd, h_next[...], NT, preferred_element_type=F32))
        start_sum(step, local_fields)
        if step + 1 < STEPS:
            exchange_pairs(step + 1, early, half)

    scale = finish_sum(STEPS - 1)
    for f in range(fields):
        cons_ref[f, STEPS - 1 : STEPS] = (scale * local_fields)[f : f + 1]
    mix = (scale - 1.0) * we_ref[...]

    def leave(b, carry):
        rows = pl.ds(b * block, block)
        out_ref[rows] = rescaled(h_next[rows], mix)
        return carry

    lax.fori_loop(0, blocks, leave, 0)

    for i in range(pieces):
        for copy in first_copies(i) + relay_copies(i):
            copy.wait_send()
        swap_copy(i).wait_send()
    for step in range(STEPS):
        wait_bytes(send.at[step, pl.ds(0, n_patch - 1)], as_sem.at[step])
        wait_bytes(ar_all.at[step, pl.ds(0, half - 1)], ps_sem.at[step])
        wait_bytes(ax_all.at[step, pl.ds(0, plane - 1)], xs_sem.at[step])


def shards(
    n_patch,
    n_feat,
    latents,
    neighbours,
    degree,
    send_rows,
    area,
    scenario,
    totals,
    w_send,
    w_recv,
    b_edge,
    w_msg,
    w_node,
    w_out,
    gain,
    w_dec,
    w_enc,
):
    nodes, width = latents.shape
    deg, slot = neighbours.shape[1], send_rows.shape[1]
    fields = w_dec.shape[0]
    block = min(256, nodes)
    blocks = nodes // block
    few = 32
    groups = nodes // few
    remote = n_patch * slot
    pieces = 6
    parts = 4
    lanes = 128
    sides = max(n_feat, 2)
    vmem = pl.BlockSpec(memory_space=pltpu.VMEM)
    smem = pl.BlockSpec(memory_space=pltpu.SMEM)
    hbm = pl.BlockSpec(memory_space=pltpu.HBM)
    dma = pltpu.SemaphoreType.DMA
    final, conserved = pl.pallas_call(
        functools.partial(kernel, n_patch, n_feat),
        out_shape=(
            jax.ShapeDtypeStruct((nodes, width), BF16),
            jax.ShapeDtypeStruct((fields, STEPS, nodes), F32),
        ),
        in_specs=[hbm, vmem, vmem, vmem, vmem, smem, vmem, hbm, hbm, vmem, hbm, hbm, hbm]
        + [vmem] * 3,
        out_specs=(vmem, vmem),
        scratch_shapes=[
            pltpu.VMEM((pieces, width, width), BF16),
            pltpu.VMEM((nodes, deg), jnp.int32),
            pltpu.VMEM((remote, nodes), BF16),
            pltpu.VMEM((groups, deg * few, nodes), BF16),
            pltpu.VMEM((groups, deg * few, remote), BF16),
            pltpu.VMEM((groups, deg * few, width), F32),
            pltpu.VMEM((nodes + remote, width), BF16),
            pltpu.VMEM((nodes, width), F32),
            pltpu.VMEM((blocks, block, width), F32),
            pltpu.VMEM((nodes, width), BF16),
            pltpu.VMEM((nodes, width), BF16),
            pltpu.VMEM((STEPS, n_patch, slot, width), BF16),
            pltpu.VMEM((STEPS, n_patch, slot, width), BF16),
            pltpu.VMEM((STEPS, 1, lanes), F32),
            pltpu.VMEM((STEPS, n_patch // 2, 1, lanes), F32),
            pltpu.VMEM((STEPS, 1, lanes), F32),
            pltpu.VMEM((STEPS, 2 * n_feat, 1, lanes), F32),
            pltpu.SemaphoreType.REGULAR((n_patch,)),
            pltpu.SemaphoreType.REGULAR,
            dma,
            dma((pieces,)),
            dma((pieces, sides)),
            dma((pieces, sides)),
            dma((pieces,)),
            dma((pieces,)),
            dma((STEPS,)),
            dma((STEPS, parts)),
            dma((STEPS,)),
            dma((STEPS,)),
            dma((STEPS,)),
            dma((STEPS,)),
        ],
        compiler_params=pltpu.CompilerParams(
            collective_id=0, has_side_effects=True, vmem_limit_bytes=63 * 1024 * 1024
        ),
    )(
        latents,
        neighbours.T,
        degree,
        send_rows.T,
        area,
        scenario,
        totals.T,
        w_send,
        w_recv,
        b_edge,
        w_msg,
        w_node,
        w_out,
        gain,
        w_dec,
        w_enc,
    )
    return final, jnp.transpose(conserved, (1, 0, 2))


def solution(mesh):
    every = ("members", "patch", "feat")
    group = ("patch", "feat")
    column = P(None, None, "feat")
    return jax.shard_map(
        functools.partial(shards, mesh.shape["patch"], mesh.shape["feat"]),
        mesh=mesh,
        in_specs=(
            P(every, None),
            P(group, None),
            P(group),
            P(group, None),
            P(group),
            P("members"),
            P(),
            column,
            column,
            P(),
            column,
            column,
            column,
            P(),
            P(),
            P(),
        ),
        out_specs=(P(every, None), P("members", None, group)),
        check_vma=False,
    )
```

time: 195 us -> 189 us (0.969)
  local copies, waits for them, and re-layouts: 6.03 us -> 2.68 us
  Pallas kernels: 188 us -> 185 us
    pallas_call x1, Pallas kernels: 188 us -> 185 us  [shards(): pl.pallas_call(functools.partial(kernel, n_patch, n_feat), out_shape=(jax...]
where the time goes in v2:
time: 189 us
  Pallas kernels  185 us (98%)
  local copies, waits for them, and re-layouts  2.68 us (1%)
    pallas_call x1, Pallas kernels, shards(): pl.pallas_call(functools.partial(kernel, n_patch, n_feat), out_shape=(jax...  185 us

profile of v2, /device:TPU:33, one launch (start us, length us, event | category | flops | bytes accessed | tf_op | source)
XLA Modules:
  0.0 188.6 jit_solution(6315519405569701941)
XLA Ops:
  0.6 185.3 %shard_map.167 = (bf16[768,512]{1,0:T(8,128)(2,1)}, f32[3,2,768]{2,1,0:T(2,128)}) custom-call(bf16[768,512]{1,0:T(8,128)(2,1)} %h_ref.1, s32[8,768]{1,0:T(8,128)} %bitcast.4, s32[768]{0:T(1024)} %deg_ref.1, s32[8,64]{1,0:T(8,128)} %bitcast.6, f32[768]{0:T(1024)} %area_ref.1, s32[3]{0:T(128)} %scen_ref.1, f32[3,16]{1,0:T(4,128)} %bitcast.7, ...), custom_call_target="tpu_custom_call" | custom-call | tf_op jit(solution)/shard_map/pallas_call | solution.py:549
  186.0 0.0 copy-start
  186.0 2.1 %copy.20 = bf16[768,512]{1,0:T(8,128)(2,1)} copy(bf16[768,512]{1,0:T(8,128)(2,1)} %get-tuple-element.8) | data formatting | bytes 1572864
  188.0 0.0 copy-done
  188.0 0.6 copy.21
Async XLA Ops:
  186.0 2.1 %copy-start = (f32[3,2,768]{2,1,0:T(2,128)S(1)}, f32[3,2,768]{2,1,0:T(2,128)}, u32[]{:S(2)}) copy-start(f32[3,2,768]{2,1,0:T(2,128)} %get-tuple-element.5) | copy-start | bytes 55300

commit v3 on v2

--- a/solution.py
+++ b/solution.py
@@ -48,6 +48,7 @@
     wd_ref,
     we_ref,
     out_ref,
+    change_ref,
     cons_ref,
     w,
     ids,
@@ -68,7 +69,9 @@
     ax_all,
     in_sem,
     token_sem,
+    pair_sem,
     h_sem,
+    out_sem,
     wl_sem,
     ws_sem,
     wr_sem,
@@ -88,7 +91,6 @@
     few = packed // deg
     blocks, block = h_node.shape[0], h_node.shape[1]
     cols = ws_ref.shape[2]
-    half = n_patch // 2
     parts = ar_sem.shape[1]
     part_slots = n_patch // parts
     remote = n_patch * slot
@@ -106,12 +108,28 @@
         return lax.rem(feat + offset, n_feat)
 
     rank = lax.rem(me + n_patch - 1, n_patch)
-    ahead = peer(1)
-    behind = peer(n_patch - 1)
+    half = n_patch // 2
+    depth = lax.div(me, 2)
+    ahead = peer(2)
+    behind = peer(n_patch - 2)
+    first = jnp.where(core == 1, 0, 1)
+    last = jnp.where(core == 1, half - 1, 0)
+    paired = depth > 0
     barrier = pltpu.get_barrier_semaphore()
-    pl.semaphore_signal(barrier, inc=1, device_id={"patch": behind}, device_id_type=MESH)
+
+    def greet(**device):
+        pl.semaphore_signal(barrier, inc=1, device_id=device, device_id_type=MESH)
+
+    @pl.when(depth != first)
+    def _():
+        greet(patch=behind)
+
+    @pl.when(paired)
+    def _():
+        greet(patch=partner)
+
     for offset in range(1, n_feat):
-        pl.semaphore_signal(barrier, inc=1, device_id={"feat": side(offset)}, device_id_type=MESH)
+        greet(feat=side(offset))
 
     span = width // 2
     mine = pl.ds(pl.multiple_of(core * span, span), span)
@@ -141,15 +159,29 @@
     for i in range(2, pieces):
         local[i].start()
 
-    pl.semaphore_wait(barrier, n_feat)
-
-    @pl.when(rank > 0)
+    greetings = n_feat - 1 + jnp.where(depth != last, 1, 0) + jnp.where(paired, 1, 0)
+    pl.semaphore_wait(barrier, greetings)
+    closing = me == n_patch - 2
+
+    def tell_ahead():
+        pl.semaphore_signal(token_sem, inc=1, device_id={"patch": ahead}, device_id_type=MESH)
+
+    @pl.when(depth != first)
     def _():
         pl.semaphore_wait(token_sem, 1)
 
-    @pl.when(rank < n_patch - 1)
+    @pl.when(jnp.logical_and(depth != last, jnp.logical_not(closing)))
     def _():
-        pl.semaphore_signal(token_sem, inc=1, device_id={"patch": ahead}, device_id_type=MESH)
+        tell_ahead()
+
+    @pl.when(paired)
+    def _():
+        pl.semaphore_signal(pair_sem, inc=1, device_id={"patch": partner}, device_id_type=MESH)
+        pl.semaphore_wait(pair_sem, 1)
+
+    @pl.when(closing)
+    def _():
+        tell_ahead()
 
     def arrive(back, carry):
         pl.semaphore_signal(
@@ -257,15 +289,14 @@
             device_id_type=MESH,
         ).start()
 
-    def exchange_pairs(step, first, last):
+    def exchange_all(step):
         def body(j, carry):
             exchange(step, half - j)
             exchange(step, half + j)
             return carry
 
-        if first == 0:
-            exchange(step, half)
-        lax.fori_loop(max(first, 1), last, body, 0)
+        exchange(step, half)
+        lax.fori_loop(1, half, body, 0)
 
     def wait_part(step, g):
         count = part_slots - 1 if g == parts - 1 else part_slots
@@ -321,7 +352,6 @@
     )
     plane = 2 * n_feat
     seat = core * n_feat + feat
-    depth = lax.div(me, 2)
 
     def seat_copy(step, offset):
         other = lax.rem(seat + offset, plane)
@@ -338,20 +368,15 @@
     def wait_bytes(ref, sem):
         pltpu.make_async_copy(ref, ref, sem).wait()
 
-    def start_sum(step, local_fields):
+    def put_sum(step, local_fields):
         area = area_ref[...].reshape(1, nodes)
         part = jnp.sum(local_fields * area, axis=1, keepdims=True)
         wide = jnp.broadcast_to(part, (fields, lanes))
         line = jnp.sum(jnp.where(mark, wide, 0.0), axis=0, keepdims=True)
-        ax_src[step] = line
-        ax_all[step, pl.ds(seat, 1)] = line.reshape(1, 1, lanes)
-        for offset in range(1, plane):
-            seat_copy(step, offset).start()
-        wait_bytes(ax_all.at[step, pl.ds(0, plane - 1)], xr_sem.at[step])
-        line = jnp.sum(ax_all[step], axis=0)
         ar_src[step] = line
         ar_all[step, pl.ds(depth, 1)] = line.reshape(1, 1, lanes)
 
+    def send_sum(step):
         def one(offset):
             pltpu.make_async_remote_copy(
                 src_ref=ar_src.at[step],
@@ -375,6 +400,12 @@
     def finish_sum(step):
         wait_bytes(ar_all.at[step, pl.ds(0, half - 1)], pr_sem.at[step])
         line = jnp.sum(ar_all[step], axis=0)
+        ax_src[step] = line
+        ax_all[step, pl.ds(seat, 1)] = line.reshape(1, 1, lanes)
+        for offset in range(1, plane):
+            seat_copy(step, offset).start()
+        wait_bytes(ax_all.at[step, pl.ds(0, plane - 1)], xr_sem.at[step])
+        line = jnp.sum(ax_all[step], axis=0)
         wide = jnp.broadcast_to(line, (fields, lanes))
         integral = jnp.sum(jnp.where(mark, wide, 0.0), axis=1, keepdims=True)
         return target * nodes_all / integral
@@ -479,26 +510,22 @@
         for b in range(blocks):
             finish_block(b)
 
+        if step + 1 == STEPS:
+            give = pltpu.make_async_copy(h_next, out_ref, out_sem)
+            give.start()
+        local_fields = softplus(lax.dot_general(wd, h_next[...], NT, preferred_element_type=F32))
+        put_sum(step, local_fields)
         if step + 1 < STEPS:
             fill_send(step + 1)
-            early = half // 4
-            exchange_pairs(step + 1, 0, early)
-        local_fields = softplus(lax.dot_general(wd, h_next[...], NT, preferred_element_type=F32))
-        start_sum(step, local_fields)
+        send_sum(step)
         if step + 1 < STEPS:
-            exchange_pairs(step + 1, early, half)
+            exchange_all(step + 1)
 
     scale = finish_sum(STEPS - 1)
+    change_ref[...] = (scale - 1.0) * local_fields
     for f in range(fields):
         cons_ref[f, STEPS - 1 : STEPS] = (scale * local_fields)[f : f + 1]
-    mix = (scale - 1.0) * we_ref[...]
-
-    def leave(b, carry):
-        rows = pl.ds(b * block, block)
-        out_ref[rows] = rescaled(h_next[rows], mix)
-        return carry
-
-    lax.fori_loop(0, blocks, leave, 0)
+    give.wait()
 
     for i in range(pieces):
         for copy in first_copies(i) + relay_copies(i):
@@ -546,15 +573,16 @@
     smem = pl.BlockSpec(memory_space=pltpu.SMEM)
     hbm = pl.BlockSpec(memory_space=pltpu.HBM)
     dma = pltpu.SemaphoreType.DMA
-    final, conserved = pl.pallas_call(
+    latest, change, conserved = pl.pallas_call(
         functools.partial(kernel, n_patch, n_feat),
         out_shape=(
             jax.ShapeDtypeStruct((nodes, width), BF16),
+            jax.ShapeDtypeStruct((fields, nodes), F32),
             jax.ShapeDtypeStruct((fields, STEPS, nodes), F32),
         ),
         in_specs=[hbm, vmem, vmem, vmem, vmem, smem, vmem, hbm, hbm, vmem, hbm, hbm, hbm]
         + [vmem] * 3,
-        out_specs=(vmem, vmem),
+        out_specs=(hbm, vmem, vmem),
         scratch_shapes=[
             pltpu.VMEM((pieces, width, width), BF16),
             pltpu.VMEM((nodes, deg), jnp.int32),
@@ -575,6 +603,8 @@
             pltpu.VMEM((STEPS, 2 * n_feat, 1, lanes), F32),
             pltpu.SemaphoreType.REGULAR((n_patch,)),
             pltpu.SemaphoreType.REGULAR,
+            pltpu.SemaphoreType.REGULAR,
+            dma,
             dma,
             dma((pieces,)),
             dma((pieces, sides)),
@@ -609,6 +639,10 @@
         w_dec,
         w_enc,
     )
+    update = lax.dot_general(
+        change, w_enc, (((0,), (0,)), ((), ())), preferred_element_type=F32
+    )
+    final = (latest.astype(F32) + update).astype(BF16)
     return final, jnp.transpose(conserved, (1, 0, 2))
 
 

time: 189 us -> 189 us (level)
  matrix products: 0 us -> 2.46 us
  local copies, waits for them, and re-layouts: 2.68 us -> 0.61 us
    dot_general x0 -> x1, matrix products: none -> 2.46 us  [shards(): lax.dot_general(change, w_enc, (((0,), (0,)), ((), ())), preferred_elemen...]
    unnamed x4 -> x5, local copies, waits for them, and re-layouts: 2.68 us -> 0.61 us
where the time goes in v3:
time: 189 us
  Pallas kernels  185 us (98%)
  matrix products  2.46 us (1%)
    pallas_call x1, Pallas kernels, shards(): pl.pallas_call(functools.partial(kernel, n_patch, n_feat), out_shape=(jax...  185 us

profile of v3, /device:TPU:33, one launch (start us, length us, event | category | flops | bytes accessed | tf_op | source)
XLA Modules:
  0.0 188.9 jit_solution(6605604697588994990)
XLA Ops:
  0.6 0.0 copy-start
  0.6 185.2 %shard_map.167 = (bf16[768,512]{1,0:T(8,128)(2,1)}, f32[3,768]{1,0:T(4,128)}, f32[3,2,768]{2,1,0:T(2,128)}) custom-call(bf16[768,512]{1,0:T(8,128)(2,1)} %h_ref.1, s32[8,768]{1,0:T(8,128)} %bitcast.6, s32[768]{0:T(1024)} %deg_ref.1, s32[8,64]{1,0:T(8,128)} %bitcast.8, f32[768]{0:T(1024)} %area_ref.1, s32[3]{0:T(128)} %scen_ref.1, f32[3,16]{1,0:T(4,128)} %bitcast.9, ...), custom_call_target="tpu_custom_call" | custom-call | tf_op jit(solution)/shard_map/pallas_call | solution.py:576
  185.8 0.0 copy-done
  185.8 0.0 copy-start.1
  185.9 2.5 %add_convert_fusion = bf16[768,512]{1,0:T(8,128)(2,1)} fusion(bf16[768,512]{1,0:T(8,128)(2,1)} %get-tuple-element.5, f32[3,768]{1,0:T(4,128)} %get-tuple-element.6, f32[3,512]{1,0:T(4,128)S(1)} %copy-done), kind=kOutput, calls=%fused_computation | convolution fusion | flops 3538944 | bytes 1588224 | tf_op jit(solution)/shard_map/dot_general | solution.py:642
  188.3 0.0 copy-done.1
  188.3 0.6 copy.19
Async XLA Ops:
  0.6 185.2 %copy-start = (f32[3,512]{1,0:T(4,128)S(1)}, f32[3,512]{1,0:T(4,128)}, u32[]{:S(2)}) copy-start(f32[3,512]{1,0:T(4,128)} %we_ref.1) | copy-start | bytes 18436
  185.8 2.5 %copy-start.1 = (f32[3,2,768]{2,1,0:T(2,128)S(1)}, f32[3,2,768]{2,1,0:T(2,128)}, u32[]{:S(2)}) copy-start(f32[3,2,768]{2,1,0:T(2,128)} %get-tuple-element.7) | copy-start | bytes 55300

commit v4 on v3

--- a/solution.py
+++ b/solution.py
@@ -67,9 +67,6 @@
     ar_all,
     ax_src,
     ax_all,
-    in_sem,
-    token_sem,
-    pair_sem,
     h_sem,
     out_sem,
     wl_sem,
@@ -107,29 +104,21 @@
     def side(offset):
         return lax.rem(feat + offset, n_feat)
 
-    rank = lax.rem(me + n_patch - 1, n_patch)
     half = n_patch // 2
     depth = lax.div(me, 2)
-    ahead = peer(2)
-    behind = peer(n_patch - 2)
-    first = jnp.where(core == 1, 0, 1)
-    last = jnp.where(core == 1, half - 1, 0)
-    paired = depth > 0
     barrier = pltpu.get_barrier_semaphore()
 
-    def greet(**device):
-        pl.semaphore_signal(barrier, inc=1, device_id=device, device_id_type=MESH)
-
-    @pl.when(depth != first)
-    def _():
-        greet(patch=behind)
-
-    @pl.when(paired)
-    def _():
-        greet(patch=partner)
-
+    def greet(offset, carry):
+        pl.semaphore_signal(barrier, inc=1, device_id={"patch": peer(offset)}, device_id_type=MESH)
+        return carry
+
+    def greet_pair(j, carry):
+        return greet(half + j, greet(half - j, carry))
+
+    greet(half, 0)
+    lax.fori_loop(1, half, greet_pair, 0)
     for offset in range(1, n_feat):
-        greet(feat=side(offset))
+        pl.semaphore_signal(barrier, inc=1, device_id={"feat": side(offset)}, device_id_type=MESH)
 
     span = width // 2
     mine = pl.ds(pl.multiple_of(core * span, span), span)
@@ -159,41 +148,6 @@
     for i in range(2, pieces):
         local[i].start()
 
-    greetings = n_feat - 1 + jnp.where(depth != last, 1, 0) + jnp.where(paired, 1, 0)
-    pl.semaphore_wait(barrier, greetings)
-    closing = me == n_patch - 2
-
-    def tell_ahead():
-        pl.semaphore_signal(token_sem, inc=1, device_id={"patch": ahead}, device_id_type=MESH)
-
-    @pl.when(depth != first)
-    def _():
-        pl.semaphore_wait(token_sem, 1)
-
-    @pl.when(jnp.logical_and(depth != last, jnp.logical_not(closing)))
-    def _():
-        tell_ahead()
-
-    @pl.when(paired)
-    def _():
-        pl.semaphore_signal(pair_sem, inc=1, device_id={"patch": partner}, device_id_type=MESH)
-        pl.semaphore_wait(pair_sem, 1)
-
-    @pl.when(closing)
-    def _():
-        tell_ahead()
-
-    def arrive(back, carry):
-        pl.semaphore_signal(
-            in_sem.at[rank],
-            inc=1,
-            device_id={"patch": peer(n_patch - back)},
-            device_id_type=MESH,
-        )
-        return carry
-
-    lax.fori_loop(1, rank + 1, arrive, 0)
-
     def side_part(i, rows, owner, to, at):
         ref = w.at[i, rows, cols_of(owner)]
         return pltpu.make_async_remote_copy(
@@ -246,9 +200,6 @@
         for copy in relay_copies(i):
             copy.wait_recv()
         swap_copy(i).start()
-
-    own_out(0)
-    own_out(1)
 
     picks = rows_ref[...].T.astype(F32)
     spread = jnp.where(
@@ -303,21 +254,12 @@
         ref = recv.at[step, pl.ds(0, count)]
         pltpu.make_async_copy(ref, ref, ar_sem.at[step, g]).wait()
 
-    def send_back(back, carry):
-        exchange(0, n_patch - back)
-        return carry
-
-    def send_ahead(on, carry):
-        pl.semaphore_wait(in_sem.at[rank + on], 1)
-        exchange(0, on)
-        return carry
-
-    lax.fori_loop(1, rank + 1, send_back, 0)
+    pl.semaphore_wait(barrier, n_patch - 1 + n_feat - 1)
+    exchange_all(0)
+    for i in range(pieces):
+        own_out(i)
     pass_on(0)
     pass_on(1)
-    for i in range(2, pieces):
-        own_out(i)
-    lax.fori_loop(1, n_patch - rank, send_ahead, 0)
 
     raw = nbr_ref[...]
     far_id = jnp.maximum(raw - nodes, 0)
@@ -601,9 +543,6 @@
             pltpu.VMEM((STEPS, n_patch // 2, 1, lanes), F32),
             pltpu.VMEM((STEPS, 1, lanes), F32),
             pltpu.VMEM((STEPS, 2 * n_feat, 1, lanes), F32),
-            pltpu.SemaphoreType.REGULAR((n_patch,)),
-            pltpu.SemaphoreType.REGULAR,
-            pltpu.SemaphoreType.REGULAR,
             dma,
             dma,
             dma((pieces,)),

time: 189 us -> 189 us (level)
  no operation moved by 1% of the time
where the time goes in v4:
time: 189 us
  Pallas kernels  185 us (98%)
  matrix products  2.46 us (1%)
    pallas_call x1, Pallas kernels, shards(): pl.pallas_call(functools.partial(kernel, n_patch, n_feat), out_shape=(jax...  185 us

profile of v4, /device:TPU:33, one launch (start us, length us, event | category | flops | bytes accessed | tf_op | source)
XLA Modules:
  0.0 189.0 jit_solution(16198930980380285741)
XLA Ops:
  0.6 0.0 copy-start
  0.6 185.3 %shard_map.167 = (bf16[768,512]{1,0:T(8,128)(2,1)}, f32[3,768]{1,0:T(4,128)}, f32[3,2,768]{2,1,0:T(2,128)}) custom-call(bf16[768,512]{1,0:T(8,128)(2,1)} %h_ref.1, s32[8,768]{1,0:T(8,128)} %bitcast.6, s32[768]{0:T(1024)} %deg_ref.1, s32[8,64]{1,0:T(8,128)} %bitcast.8, f32[768]{0:T(1024)} %area_ref.1, s32[3]{0:T(128)} %scen_ref.1, f32[3,16]{1,0:T(4,128)} %bitcast.9, ...), custom_call_target="tpu_custom_call" | custom-call | tf_op jit(solution)/shard_map/pallas_call | solution.py:518
  185.9 0.0 copy-done
  185.9 0.0 copy-start.1
  185.9 2.5 %add_convert_fusion = bf16[768,512]{1,0:T(8,128)(2,1)} fusion(bf16[768,512]{1,0:T(8,128)(2,1)} %get-tuple-element.5, f32[3,768]{1,0:T(4,128)} %get-tuple-element.6, f32[3,512]{1,0:T(4,128)S(1)} %copy-done), kind=kOutput, calls=%fused_computation | convolution fusion | flops 3538944 | bytes 1588224 | tf_op jit(solution)/shard_map/dot_general | solution.py:581
  188.4 0.0 copy-done.1
  188.4 0.6 copy.19
Async XLA Ops:
  0.6 185.3 %copy-start = (f32[3,512]{1,0:T(4,128)S(1)}, f32[3,512]{1,0:T(4,128)}, u32[]{:S(2)}) copy-start(f32[3,512]{1,0:T(4,128)} %we_ref.1) | copy-start | bytes 18436
  185.9 2.5 %copy-start.1 = (f32[3,2,768]{2,1,0:T(2,128)S(1)}, f32[3,2,768]{2,1,0:T(2,128)}, u32[]{:S(2)}) copy-start(f32[3,2,768]{2,1,0:T(2,128)} %get-tuple-element.7) | copy-start | bytes 55300

commit v5 on v3

--- a/solution.py
+++ b/solution.py
@@ -183,16 +183,23 @@
     def _():
         tell_ahead()
 
-    def arrive(back, carry):
-        pl.semaphore_signal(
-            in_sem.at[rank],
-            inc=1,
-            device_id={"patch": peer(n_patch - back)},
-            device_id_type=MESH,
-        )
-        return carry
-
-    lax.fori_loop(1, rank + 1, arrive, 0)
+    def arrive(offset):
+        @pl.when(rank + offset >= n_patch)
+        def _():
+            pl.semaphore_signal(
+                in_sem.at[rank],
+                inc=1,
+                device_id={"patch": peer(offset)},
+                device_id_type=MESH,
+            )
+
+    def arrive_pair(j, carry):
+        arrive(half - j)
+        arrive(half + j)
+        return carry
+
+    arrive(half)
+    lax.fori_loop(1, half, arrive_pair, 0)
 
     def side_part(i, rows, owner, to, at):
         ref = w.at[i, rows, cols_of(owner)]
@@ -246,9 +253,6 @@
         for copy in relay_copies(i):
             copy.wait_recv()
         swap_copy(i).start()
-
-    own_out(0)
-    own_out(1)
 
     picks = rows_ref[...].T.astype(F32)
     spread = jnp.where(
@@ -273,6 +277,8 @@
 
     load_h.wait()
     fill_send(0)
+    own_out(0)
+    own_out(1)
 
     def slot_of(d):
         return jnp.where(d < 0, -2 * d - 1, 2 * d)
@@ -289,22 +295,32 @@
             device_id_type=MESH,
         ).start()
 
-    def exchange_all(step):
+    def exchange_first(step):
+        exchange(step, half)
+        exchange(step, half - 1)
+        exchange(step, half + 1)
+
+    def exchange_rest(step):
         def body(j, carry):
             exchange(step, half - j)
             exchange(step, half + j)
             return carry
 
-        exchange(step, half)
-        lax.fori_loop(1, half, body, 0)
+        lax.fori_loop(2, half, body, 0)
 
     def wait_part(step, g):
         count = part_slots - 1 if g == parts - 1 else part_slots
         ref = recv.at[step, pl.ds(0, count)]
         pltpu.make_async_copy(ref, ref, ar_sem.at[step, g]).wait()
 
-    def send_back(back, carry):
-        exchange(0, n_patch - back)
+    def send_back(offset):
+        @pl.when(rank + offset >= n_patch)
+        def _():
+            exchange(0, offset)
+
+    def send_back_pair(j, carry):
+        send_back(half - j)
+        send_back(half + j)
         return carry
 
     def send_ahead(on, carry):
@@ -312,7 +328,8 @@
         exchange(0, on)
         return carry
 
-    lax.fori_loop(1, rank + 1, send_back, 0)
+    send_back(half)
+    lax.fori_loop(1, half, send_back_pair, 0)
     pass_on(0)
     pass_on(1)
     for i in range(2, pieces):
@@ -440,10 +457,18 @@
         h_node[b] = mm(h_next[pl.ds(b * block, block)], w[2])
         return carry
 
-    def remote_edges(t, carry):
+    fan = remote // 2
+
+    def far_edges(t, carry):
         for u in range(unroll):
             g = t * unroll + u
-            found = mm(ohr[g], table[pl.ds(nodes, remote)])
+            pre[g] += mm(ohr[g, :, pl.ds(0, fan)], table[pl.ds(nodes, fan)])
+        return carry
+
+    def near_edges(t, carry):
+        for u in range(unroll):
+            g = t * unroll + u
+            found = mm(ohr[g, :, pl.ds(fan, fan)], table[pl.ds(nodes + fan, fan)])
             total = jnp.zeros((few, width), F32)
             for k in range(deg):
                 rows = pl.ds(k * few, few)
@@ -480,6 +505,9 @@
     lax.fori_loop(0, groups // unroll, local_edges, 0)
     for i in range(2, pieces):
         pass_over(i)
+    for i in range(2, pieces):
+        swap_copy(i).wait_recv()
+    lax.fori_loop(0, blocks, node_part, 0)
 
     mix = None
     for step in range(STEPS):
@@ -502,24 +530,24 @@
         for g in range(parts):
             wait_part(step, g)
             place_part(step, g, mix)
-        lax.fori_loop(0, groups // unroll, remote_edges, 0)
-        if step == 0:
-            for i in range(2, pieces):
-                swap_copy(i).wait_recv()
-            lax.fori_loop(0, blocks, node_part, 0)
+            if g == parts // 2 - 1:
+                lax.fori_loop(0, groups // unroll, far_edges, 0)
+        lax.fori_loop(0, groups // unroll, near_edges, 0)
         for b in range(blocks):
             finish_block(b)
 
         if step + 1 == STEPS:
             give = pltpu.make_async_copy(h_next, out_ref, out_sem)
             give.start()
+        else:
+            fill_send(step + 1)
         local_fields = softplus(lax.dot_general(wd, h_next[...], NT, preferred_element_type=F32))
+        if step + 1 < STEPS:
+            exchange_first(step + 1)
         put_sum(step, local_fields)
-        if step + 1 < STEPS:
-            fill_send(step + 1)
         send_sum(step)
         if step + 1 < STEPS:
-            exchange_all(step + 1)
+            exchange_rest(step + 1)
 
     scale = finish_sum(STEPS - 1)
     change_ref[...] = (scale - 1.0) * local_fields

time: 189 us -> 183 us (0.968)
  Pallas kernels: 185 us -> 179 us
    pallas_call x1, Pallas kernels: 185 us -> 179 us  [shards(): pl.pallas_call(functools.partial(kernel, n_patch, n_feat), out_shape=(jax...]
where the time goes in v5:
time: 183 us
  Pallas kernels  179 us (98%)
  matrix products  2.45 us (1%)
    pallas_call x1, Pallas kernels, shards(): pl.pallas_call(functools.partial(kernel, n_patch, n_feat), out_shape=(jax...  179 us

profile of v5, /device:TPU:33, one launch (start us, length us, event | category | flops | bytes accessed | tf_op | source)
XLA Modules:
  0.0 182.9 jit_solution(12975684410115922454)
XLA Ops:
  0.6 0.0 copy-start
  0.6 179.1 %shard_map.167 = (bf16[768,512]{1,0:T(8,128)(2,1)}, f32[3,768]{1,0:T(4,128)}, f32[3,2,768]{2,1,0:T(2,128)}) custom-call(bf16[768,512]{1,0:T(8,128)(2,1)} %h_ref.1, s32[8,768]{1,0:T(8,128)} %bitcast.6, s32[768]{0:T(1024)} %deg_ref.1, s32[8,64]{1,0:T(8,128)} %bitcast.8, f32[768]{0:T(1024)} %area_ref.1, s32[3]{0:T(128)} %scen_ref.1, f32[3,16]{1,0:T(4,128)} %bitcast.9, ...), custom_call_target="tpu_custom_call" | custom-call | tf_op jit(solution)/shard_map/pallas_call | solution.py:604
  179.8 0.0 copy-done
  179.8 0.0 copy-start.1
  179.8 2.5 %add_convert_fusion = bf16[768,512]{1,0:T(8,128)(2,1)} fusion(bf16[768,512]{1,0:T(8,128)(2,1)} %get-tuple-element.5, f32[3,768]{1,0:T(4,128)} %get-tuple-element.6, f32[3,512]{1,0:T(4,128)S(1)} %copy-done), kind=kOutput, calls=%fused_computation | convolution fusion | flops 3538944 | bytes 1588224 | tf_op jit(solution)/shard_map/dot_general | solution.py:670
  182.3 0.0 copy-done.1
  182.3 0.6 copy.19
Async XLA Ops:
  0.6 179.2 %copy-start = (f32[3,512]{1,0:T(4,128)S(1)}, f32[3,512]{1,0:T(4,128)}, u32[]{:S(2)}) copy-start(f32[3,512]{1,0:T(4,128)} %we_ref.1) | copy-start | bytes 18436
  179.8 2.5 %copy-start.1 = (f32[3,2,768]{2,1,0:T(2,128)S(1)}, f32[3,2,768]{2,1,0:T(2,128)}, u32[]{:S(2)}) copy-start(f32[3,2,768]{2,1,0:T(2,128)} %get-tuple-element.7) | copy-start | bytes 55300
